TPU v7x, 32 devices: a 4x4x1 block of a 4x4x8 slice. The times are simulated.
32 devices in a mesh: sys: 1 (over z), aux: 4 (over y), orb: 8 (over x, core).
Axes of the slice: x: 4, y: 4, z: 1, core: 2. Of those that a mesh axis runs over, the one named last changes fastest.
The devices are a block of a 4x4x8 slice.
Arguments:
- aux_ints: float32 [1344, 384, 384], P(('sys', 'aux'), 'orb')
- metric: float32 [1344, 1344], P(('sys', 'aux'))
- orbitals: float32 [4, 384, 80], P('sys')
Outputs:
- output: float32 [4, 384, 384], P('sys', 'orb', 'aux')
All inputs are finite; a program needn't handle non-finite values.
Results may differ from a plain program's by a relative error of at most 0.001.
Values are sent between devices in bfloat16 or wider.
A program may use at most 768 MiB of HBM per device.

v0:
```python
import jax
import jax.numpy as jnp
from jax import lax
from jax.sharding import PartitionSpec as P

PRECISE = lax.Precision.HIGHEST


def solution(mesh):
    def local_fock(ints_blk, metric_blk, orbitals):
        m_loc = ints_blk.shape[1]
        row_start = lax.axis_index('orb') * m_loc
        half_tr = jnp.einsum('qml,dli->qmdi', ints_blk, orbitals, precision=PRECISE, preferred_element_type=jnp.float32)
        orb_rows = lax.dynamic_slice_in_dim(orbitals, row_start, m_loc, axis=1)
        gamma_part = jnp.einsum('qmdi,dmi->dq', half_tr, orb_rows, precision=PRECISE, preferred_element_type=jnp.float32)
        gamma_raw = lax.psum(gamma_part, 'orb')
        gamma_all = lax.all_gather(gamma_raw, 'aux', axis=1, tiled=True)
        gamma_fit = jnp.einsum('dq,pq->dp', gamma_all, metric_blk, precision=PRECISE, preferred_element_type=jnp.float32)
        weight_part = jnp.dot(gamma_fit, metric_blk, precision=PRECISE, preferred_element_type=jnp.float32)
        weights = lax.psum_scatter(weight_part, 'aux', scatter_dimension=1, tiled=True)
        coulomb = jnp.einsum('dq,qmn->dmn', weights, ints_blk, precision=PRECISE, preferred_element_type=jnp.float32)
        half_all = lax.all_gather(half_tr, 'aux', axis=0, tiled=True)
        fitted = jnp.einsum('pq,qmdi->pmdi', metric_blk, half_all, precision=PRECISE, preferred_element_type=jnp.float32)
        fitted_all = lax.all_gather(fitted, 'orb', axis=1, tiled=True)
        exchange = jnp.einsum('pmdi,pndi->dmn', fitted, fitted_all, precision=PRECISE, preferred_element_type=jnp.float32)
        fock_part = 2.0 * coulomb - exchange
        return lax.psum_scatter(fock_part, 'aux', scatter_dimension=2, tiled=True)

    return jax.shard_map(local_fock, mesh=mesh, in_specs=(P(('sys', 'aux'), 'orb', None), P(('sys', 'aux'), None), P('sys', None, None)), out_specs=P('sys', 'orb', 'aux'), check_vma=False)
```

profile of v0, /device:TPU:97, one launch (start us, length us, event | category | flops | bytes accessed | tf_op | source)
XLA Modules:
  0.0 2764.5 jit_solution(16590510918443581147)
XLA Ops:
  6.5 0.0 copy-start
  6.6 0.0 all-gather.4.cloned.1.call-start
  6.6 1.2 dynamic-slice_bitcast_fusion
  7.8 0.1 copy.39
  7.9 64.2 %multiply_reduce_fusion = (f32[4,336]{0,1:T(8,128)S(1)}, f32[336,48,4,80]{3,1,2,0:T(8,128)}) fusion(f32[4,80,48]{1,2,0:T(8,128)S(1)} %copy.39, f32[4,384,80]{1,2,0:T(8,128)} %param.5, f32[336,48,384]{2,1,0:T(8,128)} %param.3), kind=kOutput, calls=%fused_computation.4 | convolution fusion | flops 23792023552 | bytes 45974784 | tf_op jit(solution)/shard_map/qml,dli->qmdi/dot_general | solution.py:13
  72.0 0.1 all-gather.4.cloned.1.call-update
  72.1 0.1 all-gather.6.cloned.1.call-start
  72.2 1114.0 %all-gather.4.cloned.1.call-done = f32[1344,48,4,80]{3,1,2,0:T(8,128)} async-done(((f32[336,48,4,80]{3,1,2,0:T(8,128)}), f32[1344,48,4,80]{3,1,2,0:T(8,128)}) %all-gather.4.cloned.1.call-update) | async-done | bytes 82575376 | tf_op jit(solution)/shard_map/all_gather | solution.py:22
  1186.2 0.0 copy-done
  1186.2 455.2 %fusion.9 = f32[336,48,4,80]{0,3,2,1:T(8,128)} fusion(f32[1344,48,4,80]{3,1,2,0:T(8,128)} %all-gather.4.cloned.1.call-done, f32[336,1344]{1,0:T(8,128)S(1)} %copy-done), kind=kOutput, calls=%fused_computation.10 | convolution fusion | flops 83235962880 | bytes 105025536 | tf_op jit(solution)/shard_map/pq,qmdi->pmdi/dot_general | solution.py:23
  1641.4 0.1 all-gather.6.cloned.1.call-update
  1641.5 0.1 reduce-scatter.7.cloned.1.call-start
  1641.6 0.1 copy.31
  1641.6 12.9 psum.7
  1654.6 9.0 all-gather
  1663.6 0.1 reshape.1
  1663.7 1.6 fusion.26
  1665.3 4.4 convolution_bitcast_fusion
  1669.8 0.1 reduce-scatter.7.cloned.1.call-update
  1669.8 0.1 reduce-scatter.9.cloned.1.call-start
  1669.9 779.5 %all-gather.6.cloned.1.call-done = f32[336,384,4,80]{0,3,2,1:T(8,128)} async-done(((f32[336,48,4,80]{0,3,2,1:T(8,128)}), f32[336,384,4,80]{0,3,2,1:T(8,128)}) %all-gather.6.cloned.1.call-update) | async-done | bytes 165150736 | tf_op jit(solution)/shard_map/all_gather | solution.py:24
  2449.4 0.0 copy-start.1
  2449.4 246.9 %fusion.13 = f32[4,48,384]{2,1,0:T(8,128)S(1)} fusion(f32[336,384,4,80]{0,3,2,1:T(8,128)} %all-gather.6.cloned.1.call-done, f32[336,48,4,80]{0,3,2,1:T(8,128)} %fusion.9), kind=kOutput, calls=%fused_computation.13 | convolution fusion | flops 23781703680 | bytes 186089472 | tf_op jit(solution)/shard_map/pmdi,pndi->dmn/dot_general | solution.py:25
  2696.3 0.0 reduce-scatter.7.cloned.1.call-done
  2696.3 26.3 fusion.21
  2722.7 5.8 copy.36
  2728.5 7.3 reshape.11
  2735.8 0.1 reduce-scatter.9.cloned.1.call-update
  2735.8 15.1 reduce-scatter.9.cloned.1.call-done
  2751.0 3.4 reshape.12
  2754.4 3.1 copy.22
  2757.5 0.0 copy-done.1
  (1 shorter events, 0.0 us)
Async XLA Ops:
  6.5 1179.6 %copy-start = (f32[336,1344]{1,0:T(8,128)S(1)}, f32[336,1344]{1,0:T(8,128)}, u32[]{:S(2)}) copy-start(f32[336,1344]{1,0:T(8,128)} %param.4) | copy-start | bytes 5419012
  6.6 1179.6 %all-gather.4.cloned.1.call-start = ((), (), s32[]{:S(2)}) async-start(), calls=%async_computation.2 | async-start | bytes 165150720 | tf_op jit(solution)/shard_map/all_gather | solution.py:22
  72.1 2377.3 %all-gather.6.cloned.1.call-start = ((), (), s32[]{:S(2)}) async-start(), calls=%async_computation.3 | async-start | bytes 212336640 | tf_op jit(solution)/shard_map/all_gather | solution.py:24
  1641.5 1054.8 %reduce-scatter.7.cloned.1.call-start = ((), (), s32[]{:S(2)}) async-start(), calls=%async_computation.4 | async-start | bytes 860160
  1669.8 1081.1 %reduce-scatter.9.cloned.1.call-start = ((), (), s32[]{:S(2)}) async-start(), calls=%async_computation.5 | async-start | bytes 491520
  2449.4 308.2 %copy-start.1 = (f32[336,1344]{1,0:T(8,128)S(1)}, f32[336,1344]{1,0:T(8,128)}, u32[]{:S(2)}) copy-start(f32[336,1344]{1,0:T(8,128)} %param.4) | copy-start | bytes 5419012
Sparse Core Ops, SparseCore 0:
  72.2 1113.8 all-gather.3
  1641.6 807.7 all-gather.5
  2451.7 15.8 reduce-scatter.6
  2736.0 14.9 reduce-scatter.8
where the time goes:
time: 2770 us; the launch traced here: 2760 us
  waiting for transfers between devices  1910 us (69%)
  matrix products  799 us (29%)
    all_gather x1, waiting for transfers between devices, local_fock(): half_all = lax.all_gather(half_tr, 'aux', axis=0, tiled=True)  1110 us
    all_gather x1, waiting for transfers between devices, local_fock(): fitted_all = lax.all_gather(fitted, 'orb', axis=1, tiled=True)  779 us
    dot_general x1, matrix products, local_fock(): jnp.einsum('pq,qmdi->pmdi', metric_blk, half_all, precision=PRECISE, pref...  455 us
    dot_general x1, matrix products, local_fock(): jnp.einsum('pmdi,pndi->dmn', fitted, fitted_all, precision=PRECISE, prefe...  247 us
    dot_general x1, matrix products, local_fock(): jnp.einsum('qml,dli->qmdi', ints_blk, orbitals, precision=PRECISE, prefer...  64.2 us
  transfers between devices with their start and end apart: 4, of which 3 were waited for; matrix products, arithmetic and copies ran while one was open for 9% of the time, Pallas kernels for 0%

commit v1 on v0

v1 whole, which is shorter than its diff:
```python
import jax
import jax.numpy as jnp
from jax import lax
from jax.experimental import pallas as pl
from jax.experimental.pallas import tpu as pltpu
from jax.sharding import PartitionSpec as P

PRECISE = lax.Precision.HIGHEST
F32 = jnp.float32
BF16 = jnp.bfloat16
MESH = pl.DeviceIdType.MESH


def exchange(x, axis, n, cid):
    def kernel(x_ref, o_ref, send_sem, recv_sem):
        me = lax.axis_index(axis)
        barrier = pltpu.get_barrier_semaphore()
        for r in range(1, n):
            pl.semaphore_signal(barrier, inc=1, device_id={axis: lax.rem(me + r, n)}, device_id_type=MESH)
        pl.semaphore_wait(barrier, n - 1)
        copies = []
        for r in range(1, n):
            to = lax.rem(me + r, n)
            copy = pltpu.make_async_remote_copy(
                src_ref=x_ref.at[to], dst_ref=o_ref.at[me], send_sem=send_sem.at[r], recv_sem=recv_sem.at[r],
                device_id={axis: to}, device_id_type=MESH)
            copy.start()
            copies.append(copy)
        for copy in copies:
            copy.wait()

    return pl.pallas_call(
        kernel,
        out_shape=jax.ShapeDtypeStruct(x.shape, x.dtype),
        in_specs=[pl.BlockSpec(memory_space=pl.ANY)],
        out_specs=pl.BlockSpec(memory_space=pl.ANY),
        scratch_shapes=[pltpu.SemaphoreType.DMA((n,)), pltpu.SemaphoreType.DMA((n,))],
        compiler_params=pltpu.CompilerParams(collective_id=cid, has_side_effects=True),
    )(x)


def solution(mesh):
    n_aux, n_orb = mesh.shape['aux'], mesh.shape['orb']

    def local_fock(ints, metric, orbitals):
        n_q, n_m, n_l = ints.shape
        n_d, _, n_i = orbitals.shape
        j, k = lax.axis_index('aux'), lax.axis_index('orb')
        half = jnp.einsum('qml,dli->dqmi', ints, orbitals, precision=PRECISE, preferred_element_type=F32)
        orb_rows = lax.dynamic_slice_in_dim(orbitals, k * n_m, n_m, axis=1)
        gamma = lax.psum(jnp.einsum('dqmi,dmi->dq', half, orb_rows, precision=PRECISE), 'orb')
        gamma = lax.all_gather(gamma, 'aux', axis=1, tiled=True)
        gamma_fit = jnp.einsum('dq,pq->dp', gamma, metric, precision=PRECISE)
        weights = lax.psum_scatter(jnp.dot(gamma_fit, metric, precision=PRECISE), 'aux', scatter_dimension=1, tiled=True)
        coul = jnp.einsum('dq,qmn->dmn', weights, ints, precision=PRECISE)
        coul = lax.psum_scatter(coul, 'aux', scatter_dimension=2, tiled=True)

        half = half.reshape(n_d, n_q, n_m * n_i)
        got = exchange(half.astype(BF16), 'aux', n_aux, 0)
        got = lax.dynamic_update_slice_in_dim(got, jnp.zeros((1,) + got.shape[1:], BF16), j, axis=0)
        own = lax.dynamic_index_in_dim(half, j, axis=0, keepdims=False)
        met = lax.all_gather(metric.astype(BF16), 'aux', axis=0, tiled=True)
        fit = jnp.einsum('qp,qx->px', metric, own, precision=PRECISE)
        fit = fit + jnp.einsum('qp,qx->px', met, got.reshape(n_aux * n_q, n_m * n_i), preferred_element_type=F32)
        n_p = fit.shape[0] // n_orb
        fit = fit.reshape(n_orb, n_p, n_m * n_i)
        all_t = exchange(fit.astype(BF16), 'orb', n_orb, 1)
        mine = lax.dynamic_index_in_dim(fit, k, axis=0, keepdims=True)
        mine_hi = lax.reduce_precision(mine, 8, 7)
        rest = mine - mine_hi
        all_t = lax.dynamic_update_slice_in_dim(all_t, mine_hi.astype(BF16), k, axis=0)
        all_t = all_t.reshape(n_orb, n_p, n_m, n_i)
        n_n = n_orb * n_m
        exch = jnp.einsum('kpmi,lpni->kmln', all_t, all_t, preferred_element_type=F32).reshape(n_n, n_n)
        side = lax.dynamic_update_slice_in_dim(
            all_t.astype(F32), (mine_hi + 0.5 * rest).reshape(1, n_p, n_m, n_i), k, axis=0)
        cross = jnp.einsum('pmi,lpni->mln', rest.reshape(n_p, n_m, n_i), side, precision=PRECISE).reshape(n_m, n_n)
        cross = lax.dynamic_update_slice_in_dim(jnp.zeros((n_n, n_n), F32), cross, k * n_m, axis=0)
        exch = exch + cross + cross.T
        exch = lax.psum_scatter(exch, 'orb', scatter_dimension=0, tiled=True)
        exch = lax.all_to_all(exch.reshape(n_m, n_aux, n_n // n_aux), 'aux', 1, 0)
        return 2.0 * coul - exch.reshape(n_d, n_m, n_n // n_aux)

    return jax.shard_map(local_fock, mesh=mesh, in_specs=(P(('sys', 'aux'), 'orb', None), P(('sys', 'aux'), None), P('sys', None, None)), out_specs=P('sys', 'orb', 'aux'), check_vma=False)
```

time: 2770 us -> 708 us (0.26)
  waiting for transfers between devices: 1910 us -> 10.7 us
  matrix products: 799 us -> 213 us
  Pallas kernels: 0 us -> 231 us
  local copies, waits for them, and re-layouts: 21.2 us -> 152 us
  other arithmetic: 0 us -> 40.5 us
    all_gather x2 -> x1, waiting for transfers between devices: 1890 us -> 0.01 us  [local_fock(): met = lax.all_gather(metric.astype(BF16), 'aux', axis=0, tiled=True)]
    dot_general x5 -> x8, matrix products: 794 us -> 209 us  [the longest x1 45.9 us: local_fock(): jnp.einsum('qml,dli->dqmi', ints, orbitals, precision=PRECISE, preferred_...]
    pallas_call x0 -> x2, Pallas kernels: none -> 231 us  [exchange(): pl.pallas_call(kernel, out_shape=jax.ShapeDtypeStruct(x.shape, x.dtype),...]
    reshape x0 -> x5, local copies, waits for them, and re-layouts: none -> 65.9 us  [the longest x1 30.7 us: local_fock(): all_t = all_t.reshape(n_orb, n_p, n_m, n_i)]
    dot_general x1 -> x4, local copies, waits for them, and re-layouts: 0.09 us -> 61.2 us  [the longest x2 36.5 us: local_fock(): jnp.einsum('pmi,lpni->mln', rest.reshape(n_p, n_m, n_i), side, precision=...]
    convert_element_type x0 -> x3, other arithmetic: none -> 33 us  [the longest x1 18.3 us: local_fock(): all_t.astype(F32)]
  transfers between devices with their start and end apart: 4 -> 5, of which waited for: 3 -> 1; matrix products, arithmetic and copies ran while one was open for 9% -> 57% of each run, Pallas kernels for 0% -> 33%
where the time goes in v1:
time: 708 us; the launch traced here: 701 us
  Pallas kernels  231 us (33%)
  matrix products  213 us (30%)
  local copies, waits for them, and re-layouts  152 us (21%)
  other arithmetic  40.5 us (6%)
  blocking collectives  36.5 us (5%)
  between operations  13.8 us (2%)
  waiting for transfers between devices  10.7 us (2%)
    pallas_call x2, Pallas kernels, exchange(): pl.pallas_call(kernel, out_shape=jax.ShapeDtypeStruct(x.shape, x.dtype),...  231 us
    dot_general x1, matrix products, local_fock(): jnp.einsum('qml,dli->dqmi', ints, orbitals, precision=PRECISE, preferred_...  45.9 us
    dot_general x1, matrix products, local_fock(): fit = jnp.einsum('qp,qx->px', metric, own, precision=PRECISE)  37.9 us
    dot_general x1, matrix products, local_fock(): jnp.einsum('pmi,lpni->mln', rest.reshape(n_p, n_m, n_i), side, precision=...  37.6 us
    dot_general x2, local copies, waits for them, and re-layouts, local_fock(): jnp.einsum('pmi,lpni->mln', rest.reshape(n_p, n_m, n_i), side, precision=...  36.5 us
    reshape x1, local copies, waits for them, and re-layouts, local_fock(): all_t = all_t.reshape(n_orb, n_p, n_m, n_i)  30.7 us
    dot_general x1, matrix products, local_fock(): coul = jnp.einsum('dq,qmn->dmn', weights, ints, precision=PRECISE)  26.3 us
    dot_general x1, matrix products, local_fock(): jnp.einsum('qp,qx->px', met, got.reshape(n_aux * n_q, n_m * n_i), preferr...  25.6 us
  transfers between devices with their start and end apart: 5, of which 1 were waited for; matrix products, arithmetic and copies ran while one was open for 57% of the time, Pallas kernels for 33%

profile of v1, /device:TPU:97, one launch (start us, length us, event | category | flops | bytes accessed | tf_op | source)
XLA Modules:
  0.0 701.2 jit_solution(10877054391680196461)
XLA Ops:
  6.6 2.7 convert_element_type.16
  9.2 0.1 all-gather.3.cloned.1.call-update
  9.3 0.1 reduce-scatter.10.cloned.1.call-start
  9.4 0.1 dynamic-slice_bitcast_fusion
  9.5 0.1 copy.38
  9.6 45.9 %fusion.2 = f32[4,80,336,48]{2,1,3,0:T(8,128)S(1)} fusion(f32[336,48,384]{2,1,0:T(8,128)} %param.3, f32[4,384,80]{1,2,0:T(8,128)S(1)} %copy-done), kind=kOutput, calls=%fused_computation.2 | convolution fusion | flops 23781703680 | bytes 45907968 | tf_op jit(solution)/shard_map/qml,dli->dqmi/dot_general | solution.py:49
  55.5 12.9 %fusion.4 = f32[4,1,336,1]{2,1,3,0:T(1,128)S(1)} fusion(f32[4,48,80,1]{2,3,1,0:T(1,128)S(1)} %copy.38, f32[4,80,336,48]{2,1,3,0:T(8,128)S(1)} %fusion.2), kind=kOutput, calls=%fused_computation.4 | convolution fusion | flops 61931520 | bytes 20710656 | tf_op jit(solution)/shard_map/dqmi,dmi->dq/dot_general | solution.py:51
  68.4 14.1 %psum.7 = f32[4,336]{1,0:T(4,128)S(1)} all-reduce(f32[4,336]{1,0:T(4,128)S(1)} %bitcast.78), channel_id=1, replica_groups=mesh['sys'=1,'aux'=4,'orb'=8] {'orb'}, use_global_device_ids=true, to_apply=%region_0.0 | all-reduce | flops 1344 | bytes 10752 | tf_op jit(solution)/shard_map/psum | solution.py:51
  82.5 22.4 %all-gather = f32[4,336,4]{1,2,0:T(4,128)S(1)} all-gather(f32[1,336,4]{1,2,0:T(4,128)S(1)} %bitcast.79), channel_id=1, replica_groups=mesh['sys'=1,'aux'=4,'orb'=8] {'aux'}, dimensions={0}, use_global_device_ids=true | all-gather | bytes 26880 | tf_op jit(solution)/shard_map/all_gather | solution.py:52
  104.9 0.1 reshape.34
  105.0 1.6 fusion.24
  106.6 4.4 convolution_bitcast_fusion
  111.0 0.1 reduce-scatter.10.cloned.1.call-update
  111.1 0.1 reduce-scatter.8.cloned.1.call-start
  111.2 18.4 %copy.26.x_ref = bf16[4,336,3840]{2,1,0:T(8,128)(2,1)} copy(f32[4,336,3840]{1,2,0:T(8,128)} %bitcast.66) | data formatting | bytes 30965760 | tf_op jit(solution)/shard_map/reshape | solution.py:58
  129.5 37.9 %fusion.11 = f32[3840,1344]{0,1:T(8,128)} fusion(f32[336,1344]{1,0:T(8,128)S(1)} %copy-done.3, f32[4,336,3840]{1,2,0:T(8,128)} %bitcast.67, s32[]{:T(128)S(6)} %select_n.16), kind=kOutput, calls=%fused_computation.12 | convolution fusion | flops 20808990720 | bytes 28348420 | tf_op jit(solution)/shard_map/qp,qx->px/dot_general | solution.py:63
  167.4 113.2 %shard_map.37 = bf16[4,336,3840]{2,1,0:T(8,128)(2,1)} custom-call(bf16[4,336,3840]{2,1,0:T(8,128)(2,1)} %copy.26.x_ref), custom_call_target="tpu_custom_call" | custom-call | tf_op jit(solution)/shard_map/pallas_call | solution.py:32
  280.7 1.7 broadcast_dynamic-update-slice_fusion
  282.4 25.6 %convolution_add_fusion = f32[3840,1344]{0,1:T(8,128)} fusion(f32[3840,1344]{0,1:T(8,128)} %fusion.11, bf16[1344,3840]{1,0:T(8,128)(2,1)} %bitcast.76, bf16[1344,1344]{1,0:T(8,128)(2,1)} %all-gather.3.cloned.1.call-done), kind=kOutput, calls=%fused_computation.9 | convolution fusion | flops 13877821440 | bytes 55222272 | tf_op jit(solution)/shard_map/qp,qx->px/dot_general | solution.py:64
  307.9 12.1 %convert_element_type.17.x_ref = bf16[8,168,3840]{2,1,0:T(8,128)(2,1)} convert(f32[8,168,3840]{2,1,0:T(8,128)} %bitcast.72) | non-fusion elementwise | flops 5160960 | bytes 30965760 | tf_op jit(solution)/shard_map/convert_element_type | solution.py:67
  320.0 3.6 reduce-precision_add_fusion
  323.6 6.0 reshape.32
  329.6 4.2 reshape.31
  333.9 6.6 copy.31
  340.4 118.2 %shard_map.38 = bf16[8,168,3840]{2,1,0:T(8,128)(2,1)} custom-call(bf16[8,168,3840]{2,1,0:T(8,128)(2,1)} %convert_element_type.17.x_ref), custom_call_target="tpu_custom_call" | custom-call | tf_op jit(solution)/shard_map/pallas_call | solution.py:32
  458.7 3.0 fusion.14
  461.6 30.7 %reshape.29 = bf16[8,168,48,80]{3,2,1,0:T(8,128)(2,1)} reshape(bf16[8,168,3840]{2,1,0:T(8,128)(2,1)} %fusion.14) | data formatting | bytes 20643840 | tf_op jit(solution)/shard_map/reshape | solution.py:72
  492.3 18.3 %convert_element_type.19 = f32[8,168,48,80]{3,2,1,0:T(8,128)} convert(bf16[8,168,48,80]{3,2,1,0:T(8,128)(2,1)} %reshape.29) | non-fusion elementwise | flops 5160960 | bytes 30965760 | tf_op jit(solution)/shard_map/convert_element_type | solution.py:76
  510.6 24.6 %copy.27 = bf16[8,48,80,168]{3,2,1,0:T(8,128)(2,1)} copy(bf16[8,48,80,168]{2,1,3,0:T(8,128)(2,1)} %bitcast.69) | data formatting | bytes 20643840 | tf_op jit(solution)/shard_map/kpmi,lpni->kmln/dot_general | solution.py:74
  535.3 20.8 %fusion.15 = f32[384,384]{1,0:T(8,128)S(1)} fusion(bf16[384,80,168]{2,1,0:T(8,128)(2,1)} %bitcast.75), kind=kOutput, calls=%fused_computation.21 | convolution fusion | flops 3963617280 | bytes 10911744 | tf_op jit(solution)/shard_map/kpmi,lpni->kmln/dot_general | solution.py:74
  556.1 2.2 constant_dynamic-update-slice_fusion
  558.3 36.4 %copy.30 = f32[8,48,80,168]{3,2,1,0:T(8,128)} copy(f32[8,48,80,168]{2,1,3,0:T(8,128)} %bitcast.70) | data formatting | bytes 41287680 | tf_op jit(solution)/shard_map/pmi,lpni->mln/dot_general | solution.py:77
  594.8 37.6 %add_dynamic-update-slice_fusion = (f32[384,384]{1,0:T(8,128)S(1)}, f32[48,384]{1,0:T(8,128)S(1)}) fusion(f32[384,384]{1,0:T(8,128)S(1)} %fusion.15, s32[]{:T(128)S(6)} %select_n.15, f32[168,48,80]{0,1,2:T(8,128)} %copy.31, f32[384,80,168]{2,1,0:T(8,128)} %bitcast.68), kind=kOutput, calls=%fused_computation.28 | convolution fusion | flops 2972731392 | bytes 23445508 | tf_op jit(solution)/shard_map/pmi,lpni->mln/dot_general | solution.py:77
  632.4 0.1 copy.33
  632.5 1.8 dynamic_update_slice.18
  634.4 0.9 bitcast_add_fusion
  635.3 0.1 reduce-scatter.8.cloned.1.call-update
  635.3 0.1 reduce-scatter.12.cloned.1.call-start
  635.4 26.3 %fusion.6 = f32[4,48,384]{2,0,1:T(4,128)S(1)} fusion(f32[336,48,384]{2,1,0:T(8,128)} %param.3, f32[336,4]{1,0:T(8,128)} %reduce-scatter.10.cloned.1.call-done), kind=kOutput, calls=%fused_computation.6 | convolution fusion | flops 297271296 | bytes 25072896 | tf_op jit(solution)/shard_map/dq,qmn->dmn/dot_general | solution.py:55
  661.8 5.8 copy.42
  667.6 7.3 %reshape.44 = f32[384,192]{1,0:T(8,128)} reshape(f32[384,48,4]{2,1,0:T(8,128)} %bitcast.71) | data formatting | bytes 589824
  675.0 1.0 broadcast_in_dim_reshape.3
  676.0 0.6 copy.34
  676.6 3.4 all-to-all-start
  680.0 10.4 %reduce-scatter.12.cloned.1.call-done = f32[96,192]{1,0:T(8,128)} async-done(((f32[384,192]{1,0:T(8,128)}), f32[96,192]{1,0:T(8,128)}) %reduce-scatter.12.cloned.1.call-update) | async-done | bytes 73744
  690.5 2.2 reshape.45
  692.6 0.9 copy.43
  693.6 0.6 copy.36
  (20 shorter events, 0.2 us)
Async XLA Ops:
  6.5 2.8 copy-start
  6.6 275.8 %all-gather.3.cloned.1.call-start = ((), (), s32[]{:S(2)}) async-start(), calls=%async_computation.4 | async-start | bytes 4730880 | tf_op jit(solution)/shard_map/all_gather | solution.py:62
  9.3 626.2 %reduce-scatter.10.cloned.1.call-start = ((), (), s32[]{:S(2)}) async-start(), calls=%async_computation.6 | async-start | bytes 860160
  55.5 12.9 %copy-start.2 = (f32[4,80,336,48]{2,1,3,0:T(8,128)}, f32[4,80,336,48]{2,1,3,0:T(8,128)S(1)}, u32[]{:S(2)}) copy-start(f32[4,80,336,48]{2,1,3,0:T(8,128)S(1)} %fusion.2) | copy-start | bytes 61931524
  55.5 49.5 %copy-start.3 = (f32[336,1344]{1,0:T(8,128)S(1)}, f32[336,1344]{1,0:T(8,128)}, u32[]{:S(2)}) copy-start(f32[336,1344]{1,0:T(8,128)} %param.4) | copy-start | bytes 5419012
  111.1 563.9 %reduce-scatter.8.cloned.1.call-start = ((), (), s32[]{:S(2)}) async-start(), calls=%async_computation.5 | async-start | bytes 663552 | tf_op jit(solution)/shard_map/reduce_scatter | solution.py:80
  535.3 20.9 %copy-start.4 = (f32[1,168,48,80]{3,2,1,0:T(8,128)S(1)}, f32[1,168,48,80]{3,2,1,0:T(8,128)}, u32[]{:S(2)}) copy-start(f32[1,168,48,80]{3,2,1,0:T(8,128)} %reshape.32) | copy-start | bytes 7741444
  635.3 55.1 %reduce-scatter.12.cloned.1.call-start = ((), (), s32[]{:S(2)}) async-start(), calls=%async_computation.7 | async-start | bytes 491520
  661.7 32.5 %copy-start.1 = (f32[4,384,80]{1,2,0:T(8,128)S(1)}, f32[4,384,80]{1,2,0:T(8,128)}, u32[]{:S(2)}) copy-start(f32[4,384,80]{1,2,0:T(8,128)} %param.5) | copy-start | bytes 1474564
  676.6 16.9 %all-to-all-start = ((f32[1,48,4,96]{3,1,0,2:T(8,128)}), f32[1,48,4,96]{3,1,0,2:T(8,128)S(1)}, u32[]{:S(2)}, u32[]{:S(2)}) async-start(f32[1,48,4,96]{3,1,0,2:T(8,128)} %copy.34), calls=%async_computation.1 | async-start | bytes 196608 | tf_op jit(solution)/shard_map/all_to_all | solution.py:81
Sparse Core Ops, SparseCore 0:
  9.4 45.7 all-gather.2
  111.2 21.0 reduce-scatter.9
  635.5 24.7 reduce-scatter.7
  675.1 15.3 reduce-scatter.11
